TPU v7x, 128 devices: a whole 4x4x4 slice. The times are simulated.
128 devices in a mesh: dp: 32 (over x, y, core), mp: 4 (over z).
Axes of the slice: x: 4, y: 4, z: 4, core: 2. Of those that a mesh axis runs over, the one named last changes fastest.
Arguments:
- grad_parts: bfloat16 [32, 4, 1024, 4096], P('dp', None, None, 'mp'), may hold values from -4000 to 4000
- master: float32 [4, 1024, 4096], P(None, 'dp', 'mp'), may hold values from -6 to 6
- first_moment: float32 [4, 1024, 4096], P(None, 'dp', 'mp'), may hold values from -4 to 4
- second_moment: float32 [4, 1024, 4096], P(None, 'dp', 'mp'), may hold values from 0.25 to 4
- left_basis: bfloat16 [4, 1024, 4096], P(None, 'dp', 'mp'), may hold values from -1 to 1, as said below
- right_basis: bfloat16 [4, 1024, 4096], P(None, 'dp', 'mp'), may hold values from -1 to 1, as said below
Outputs:
- weights: bfloat16 [4, 1024, 4096], P(None, None, 'mp')
- new_master: float32 [4, 1024, 4096], P(None, 'dp', 'mp')
- new_first: float32 [4, 1024, 4096], P(None, 'dp', 'mp')
- new_second: float32 [4, 1024, 4096], P(None, 'dp', 'mp')
Inputs may be any that keep to these rules, and one draw needn't show every extreme that they name: Each block left_basis[i, :, j * 1024 : (j + 1) * 1024] is an orthogonal 1024 x 1024 matrix up to rounding. Each block right_basis[i, :, j * 1024 : (j + 1) * 1024] is an orthogonal 1024 x 1024 matrix up to rounding.
All inputs are finite; a program needn't handle non-finite values.
Results may differ from a plain program's by a relative error of at most 0.02.
Values may be sent and summed in bfloat16 or wider, within the bound.
No kernel may reach another device: no remote copies, remote signals or barrier semaphores. Data moves between devices by JAX's collectives and lax.ppermute only.
A program may use at most 128 MiB of HBM per device.

v0:
```python
import jax
import jax.numpy as jnp
from jax import lax
from jax.sharding import Mesh
from jax.sharding import PartitionSpec as P

D = 4096
STEP = 10
DP = ("dp_0", "dp_1", "dp_2")
DP_MP = ("dp_0", "dp_1", "dp_2", "mp")
beta_one = 0.95
beta_two = 0.95
epsilon = 1e-08
norm_epsilon = 1e-06
learning_rate = 0.3
decay_rate = 0.1


def over_axes(array, axes):
    for axis in axes:
        array = lax.psum(array, axis)
    return array


def split_up(array, dim, peers):
    before, after = (array.shape[:dim], array.shape[dim + 1 :])
    return jnp.moveaxis(array.reshape(*before, peers, -1, *after), dim, 0)


def summed_rows(array, chips, core, dim):
    sizes = (lax.axis_size(chips), lax.axis_size(core))
    parts = split_up(array, dim, sizes[0] * sizes[1])
    inside = parts.shape[1:]
    parts = parts.reshape(*sizes, *inside).swapaxes(0, 1).reshape(-1, *inside)
    parts = lax.psum_scatter(parts, core, scatter_dimension=0, tiled=True)
    return lax.psum_scatter(parts, chips, scatter_dimension=0, tiled=True)[0]


def per_device(grad_parts, master, first_moment, second_moment, left_basis, right_basis):
    gradient = lax.psum_scatter(grad_parts[0], DP, scatter_dimension=1, tiled=True).astype(
        jnp.float32
    )
    squares_sum = over_axes(jnp.sum(gradient * gradient), DP_MP)
    clip_scale = jnp.minimum(1.0, 2.0 * D / jnp.sqrt(squares_sum + norm_epsilon))
    grad_low = gradient.astype(jnp.bfloat16)
    right_full = lax.all_gather(right_basis, DP, axis=1, tiled=True)
    turned = jnp.einsum(
        "isk,ikb->isb", grad_low, right_full, preferred_element_type=jnp.float32
    ).astype(jnp.bfloat16)
    left_cols = left_basis
    raw_term = jnp.einsum("isx,isb->xib", left_cols, turned, preferred_element_type=jnp.float32)
    rotated_rows = summed_rows(
        lax.optimization_barrier(raw_term.astype(jnp.bfloat16))
        .astype(jnp.float32)
        .astype(jnp.bfloat16),
        ("dp_0", "dp_1"),
        "dp_2",
        0,
    ).astype(jnp.float32)
    rotated = jnp.transpose(rotated_rows, (1, 0, 2))
    clipped = clip_scale * rotated
    new_first = beta_one * first_moment + (1.0 - beta_one) * clipped
    new_second = beta_two * second_moment + (1.0 - beta_two) * clipped * clipped
    bias_one = 1.0 - beta_one**STEP
    bias_two = 1.0 - beta_two**STEP
    direction = (new_first / bias_one / (jnp.sqrt(new_second / bias_two) + epsilon)).astype(
        jnp.bfloat16
    )
    back_rows = jnp.einsum(
        "isb,icb->isc", direction, right_full, preferred_element_type=jnp.float32
    ).astype(jnp.bfloat16)
    left_cols = left_basis
    update = jnp.einsum(
        "isk,ikc->isc",
        left_cols,
        lax.all_gather(back_rows, DP, axis=1, tiled=True),
        preferred_element_type=jnp.float32,
    )
    new_master = master * (1.0 - learning_rate * decay_rate) - learning_rate * update
    weights = lax.all_gather(new_master.astype(jnp.bfloat16), DP, axis=1, tiled=True)
    return (weights, new_master, new_first, new_second)


def solution(mesh):
    finer = Mesh(mesh.devices.reshape(4, 4, 2, mesh.shape["mp"]), ("dp_0", "dp_1", "dp_2", "mp"))
    placed = (
        P(DP, None, None, "mp"),
        P(None, DP, "mp"),
        P(None, DP, "mp"),
        P(None, DP, "mp"),
        P(None, DP, "mp"),
        P(None, DP, "mp"),
    )
    return jax.shard_map(
        per_device,
        mesh=finer,
        in_specs=placed,
        out_specs=(P(None, None, "mp"), P(None, DP, "mp"), P(None, DP, "mp"), P(None, DP, "mp")),
        check_vma=False,
    )
```

profile of v0, /device:TPU:1, one launch (start us, length us, event | category | flops | bytes accessed | tf_op | source)
XLA Modules:
  0.0 428.3 jit_solution(16834403755977702970)
XLA Ops:
  7.2 0.7 reduce-scatter.6.cloned.1.call-update
  8.0 0.7 all-gather.4.cloned.1.call-update
  8.7 0.0 reduce-scatter.8.cloned.1.call-start
  8.7 97.1 %reduce-scatter.6.cloned.1.call-done = bf16[4,32,1024]{2,1,0:T(8,128)(2,1)} async-done(((bf16[4,1024,1024]{2,1,0:T(8,128)(2,1)}), bf16[4,32,1024]{2,1,0:T(8,128)(2,1)}) %reduce-scatter.6.cloned.1.call-update) | async-done | bytes 262160 | tf_op jit(solution)/shard_map/reduce_scatter | solution.py:40
  105.8 56.5 %all-gather.4.cloned.1.call-done = bf16[4,1024,1024]{2,1,0:T(8,128)(2,1)} async-done(((bf16[4,32,1024]{2,1,0:T(8,128)(2,1)}), bf16[4,1024,1024]{2,1,0:T(8,128)(2,1)}) %all-gather.4.cloned.1.call-update) | async-done | bytes 8388624 | tf_op jit(solution)/shard_map/all_gather | solution.py:46
  162.3 10.8 %convert_bitcast_fusion = bf16[1024,4,1024]{0,2,1:T(8,128)(2,1)} fusion(bf16[4,32,1024]{2,1,0:T(8,128)(2,1)S(1)} %copy-done, bf16[4,32,1024]{2,1,0:T(8,128)(2,1)} %reduce-scatter.6.cloned.1.call-done, bf16[4,1024,1024]{2,1,0:T(8,128)(2,1)} %all-gather.4.cloned.1.call-done), kind=kOutput, calls=%fused_computation | convolution fusion | flops 541196288 | bytes 17301504 | tf_op jit(solution)/shard_map/isx,isb->xib/dot_general | solution.py:51
  173.2 11.4 %copy.14 = bf16[1024,4,1024]{2,0,1:T(8,128)(2,1)} copy(bf16[1024,4,1024]{0,2,1:T(8,128)(2,1)} %convert_bitcast_fusion) | data formatting | bytes 16777216 | tf_op jit(solution)/shard_map/optimization_barrier | solution.py:53
  184.6 8.6 %copy.15 = bf16[2,16,32,4,1024]{4,2,3,1,0:T(8,128)(2,1)} copy(bf16[2,16,32,4,1024]{4,2,0,1,3:T(8,128)(2,1)} %bitcast.24) | data formatting | bytes 16777216 | tf_op jit(solution)/shard_map/transpose | solution.py:34
  193.3 0.0 reduce-scatter.10.cloned.1.call-start
  193.3 18.8 %reduce-scatter.8.cloned.1.call-done = bf16[16,32,4,1024]{3,1,2,0:T(8,128)(2,1)} async-done(((bf16[32,32,4,1024]{3,1,2,0:T(8,128)(2,1)}), bf16[16,32,4,1024]{3,1,2,0:T(8,128)(2,1)}) %reduce-scatter.8.cloned.1.call-update) | async-done | bytes 4194320 | tf_op jit(solution)/shard_map/reduce_scatter | solution.py:35
  212.1 0.0 all-gather.6.cloned.1.call-start
  212.2 0.7 multiply_reduce_fusion
  212.9 9.1 %psum.28 = f32[]{:T(128)} all-reduce(f32[]{:T(128)} %multiply_reduce_fusion), channel_id=1, replica_groups=mesh['dp_0'=4,'dp_1'=4,'dp_2'=2,'mp'=4] {'dp_0'}, use_global_device_ids=true, to_apply=%region_2.0 | all-reduce | flops 1 | bytes 8 | tf_op jit(solution)/shard_map/psum | solution.py:21
  222.0 9.5 %psum.29 = f32[]{:T(128)} all-reduce(f32[]{:T(128)} %psum.28), channel_id=1, replica_groups=mesh['dp_0'=4,'dp_1'=4,'dp_2'=2,'mp'=4] {'dp_1'}, use_global_device_ids=true, to_apply=%region_3.0 | all-reduce | flops 1 | bytes 8 | tf_op jit(solution)/shard_map/psum | solution.py:21
  231.5 6.7 %psum.30 = f32[]{:T(128)} all-reduce(f32[]{:T(128)} %psum.29), channel_id=1, replica_groups=mesh['dp_0'=4,'dp_1'=4,'dp_2'=2,'mp'=4] {'dp_2'}, use_global_device_ids=true, to_apply=%region_4.0 | all-reduce | flops 1 | bytes 8 | tf_op jit(solution)/shard_map/psum | solution.py:21
  238.2 9.5 %psum.31 = f32[]{:T(128)} all-reduce(f32[]{:T(128)} %psum.30), channel_id=1, replica_groups=mesh['dp_0'=4,'dp_1'=4,'dp_2'=2,'mp'=4] {'mp'}, use_global_device_ids=true, to_apply=%region_5.0 | all-reduce | flops 1 | bytes 8 | tf_op jit(solution)/shard_map/psum | solution.py:21
  248.4 44.5 %reduce-scatter.10.cloned.1.call-done = bf16[1,32,4,1024]{3,1,2,0:T(8,128)(2,1)} async-done(((bf16[16,32,4,1024]{3,1,2,0:T(8,128)(2,1)}), bf16[1,32,4,1024]{3,1,2,0:T(8,128)(2,1)}) %reduce-scatter.10.cloned.1.call-update) | async-done | bytes 262160
  293.0 1.1 multiply_add_fusion
  294.1 7.0 %convolution_convert_fusion = bf16[4,32,1024]{2,1,0:T(8,128)(2,1)} fusion(bf16[4,1024,1024]{2,1,0:T(8,128)(2,1)} %all-gather.4.cloned.1.call-done, f32[4,32,1024]{2,1,0:T(8,128)S(1)} %get-tuple-element.15, f32[4,32,1024]{2,1,0:T(8,128)S(1)} %get-tuple-element.14), kind=kOutput, calls=%fused_computation.4 | convolution fusion | flops 269221888 | bytes 9699328 | tf_op jit(solution)/shard_map/isb,icb->isc/dot_general | solution.py:69
  301.2 0.0 all-gather.8.cloned.1.call-start
  301.2 54.2 %all-gather.6.cloned.1.call-done = bf16[4,1024,1024]{2,1,0:T(8,128)(2,1)} async-done(((bf16[4,32,1024]{2,1,0:T(8,128)(2,1)}), bf16[4,1024,1024]{2,1,0:T(8,128)(2,1)}) %all-gather.6.cloned.1.call-update) | async-done | bytes 8388624 | tf_op jit(solution)/shard_map/all_gather | solution.py:76
  355.4 5.8 %fusion.7 = (bf16[4,32,1024]{2,1,0:T(8,128)(2,1)}, f32[4,32,1024]{2,1,0:T(8,128)}) fusion(bf16[4,32,1024]{2,1,0:T(8,128)(2,1)S(1)} %copy-done, bf16[4,1024,1024]{2,1,0:T(8,128)(2,1)} %all-gather.6.cloned.1.call-done, f32[4,32,1024]{2,1,0:T(8,128)S(1)} %copy-done.6), kind=kOutput, calls=%fused_computation.16 | convolution fusion | flops 268959744 | bytes 9961472 | tf_op jit(solution)/shard_map/isk,ikc->isc/dot_general | solution.py:73
  361.3 52.4 %all-gather.8.cloned.1.call-done = bf16[4,1024,1024]{2,1,0:T(8,128)(2,1)} async-done(((bf16[4,32,1024]{2,1,0:T(8,128)(2,1)}), bf16[4,1024,1024]{2,1,0:T(8,128)(2,1)}) %all-gather.8.cloned.1.call-update) | async-done | bytes 8388624 | tf_op jit(solution)/shard_map/all_gather | solution.py:80
  413.7 7.8 %copy.17 = bf16[4,1024,1024]{2,1,0:T(8,128)(2,1)} copy(bf16[4,1024,1024]{2,1,0:T(8,128)(2,1)} %all-gather.8.cloned.1.call-done) | data formatting | bytes 16777216
  (20 shorter events, 0.2 us)
Async XLA Ops:
  7.2 155.2 %copy-start = (bf16[4,32,1024]{2,1,0:T(8,128)(2,1)S(1)}, bf16[4,32,1024]{2,1,0:T(8,128)(2,1)}, u32[]{:S(2)}) copy-start(bf16[4,32,1024]{2,1,0:T(8,128)(2,1)} %param.10) | copy-start | bytes 786436
  7.2 98.6 %reduce-scatter.6.cloned.1.call-start = ((), (), s32[]{:S(2)}) async-start(), calls=%async_computation.3 | async-start | bytes 8650752 | tf_op jit(solution)/shard_map/reduce_scatter | solution.py:40
  7.9 154.4 %all-gather.4.cloned.1.call-start = ((), (), s32[]{:S(2)}) async-start(), calls=%async_computation.4 | async-start | bytes 8650752 | tf_op jit(solution)/shard_map/all_gather | solution.py:46
  8.7 203.4 %reduce-scatter.8.cloned.1.call-start = ((), (), s32[]{:S(2)}) async-start(), calls=%async_computation.5 | async-start | bytes 12582912 | tf_op jit(solution)/shard_map/reduce_scatter | solution.py:35
  193.2 19.0 %copy-start.3 = (bf16[4,32,1024]{2,1,0:T(8,128)(2,1)S(1)}, bf16[4,32,1024]{2,1,0:T(8,128)(2,1)}, u32[]{:S(2)}) copy-start(bf16[4,32,1024]{2,1,0:T(8,128)(2,1)} %reduce-scatter.6.cloned.1.call-done) | copy-start | bytes 786436
  193.2 99.7 %copy-start.4 = (f32[4,32,1024]{2,1,0:T(8,128)S(1)}, f32[4,32,1024]{2,1,0:T(8,128)}, u32[]{:S(2)}) copy-start(f32[4,32,1024]{2,1,0:T(8,128)} %param.8) | copy-start | bytes 1572868
  193.2 99.7 %copy-start.5 = (f32[4,32,1024]{2,1,0:T(8,128)S(1)}, f32[4,32,1024]{2,1,0:T(8,128)}, u32[]{:S(2)}) copy-start(f32[4,32,1024]{2,1,0:T(8,128)} %param.9) | copy-start | bytes 1572868
  193.3 99.7 %reduce-scatter.10.cloned.1.call-start = ((), (), s32[]{:S(2)}) async-start(), calls=%async_computation.8 | async-start | bytes 4456448
  212.1 143.3 %copy-start.6 = (f32[4,32,1024]{2,1,0:T(8,128)S(1)}, f32[4,32,1024]{2,1,0:T(8,128)}, u32[]{:S(2)}) copy-start(f32[4,32,1024]{2,1,0:T(8,128)} %param.7) | copy-start | bytes 1572868
  212.1 143.3 %all-gather.6.cloned.1.call-start = ((), (), s32[]{:S(2)}) async-start(), calls=%async_computation.6 | async-start | bytes 8650752 | tf_op jit(solution)/shard_map/all_gather | solution.py:76
  294.1 67.1 %copy-start.1 = (f32[4,32,1024]{2,1,0:T(8,128)}, f32[4,32,1024]{2,1,0:T(8,128)S(1)}, u32[]{:S(2)}) copy-start(f32[4,32,1024]{2,1,0:T(8,128)S(1)} %get-tuple-element.14) | copy-start | bytes 1572868
  294.1 67.1 %copy-start.2 = (f32[4,32,1024]{2,1,0:T(8,128)}, f32[4,32,1024]{2,1,0:T(8,128)S(1)}, u32[]{:S(2)}) copy-start(f32[4,32,1024]{2,1,0:T(8,128)S(1)} %get-tuple-element.15) | copy-start | bytes 1572868
  301.2 112.5 %all-gather.8.cloned.1.call-start = ((), (), s32[]{:S(2)}) async-start(), calls=%async_computation.7 | async-start | bytes 8650752 | tf_op jit(solution)/shard_map/all_gather | solution.py:80
Sparse Core Ops, SparseCore 0:
  11.7 94.0 reduce-scatter.5
  108.2 54.1 all-gather.3
  193.4 18.6 reduce-scatter.7
  215.3 77.5 reduce-scatter.9
  301.3 54.0 all-gather.5
  361.4 52.2 all-gather.7
where the time goes:
time: 429 us; the launch traced here: 428 us
  waiting for transfers between devices  325 us (76%)
  blocking collectives  34.8 us (8%)
  local copies, waits for them, and re-layouts  27.8 us (6%)
  matrix products  23.7 us (6%)
  between operations  14.9 us (3%)
    reduce_scatter x1, waiting for transfers between devices, per_device(): lax.psum_scatter(grad_parts[0], DP, scatter_dimension=1, tiled=True)  97.1 us
    all_gather x1, waiting for transfers between devices, per_device(): right_full = lax.all_gather(right_basis, DP, axis=1, tiled=True)  56.5 us
    all_gather x1, waiting for transfers between devices, per_device(): lax.all_gather(back_rows, DP, axis=1, tiled=True)  54.2 us
    all_gather x1, waiting for transfers between devices, per_device(): lax.all_gather(new_master.astype(jnp.bfloat16), DP, axis=1, tiled=True)  52.4 us
    unnamed x7, waiting for transfers between devices  46 us
    psum x4, blocking collectives, over_axes(): array = lax.psum(array, axis)  34.8 us
    reduce_scatter x1, waiting for transfers between devices, summed_rows(): parts = lax.psum_scatter(parts, core, scatter_dimension=0, tiled=True)  18.8 us
    optimization_barrier x1, local copies, waits for them, and re-layouts, per_device(): lax.optimization_barrier(raw_term.astype(jnp.bfloat16)).astype(jnp.float32)  11.4 us
  transfers between devices with their start and end apart: 6, of which 6 were waited for; matrix products, arithmetic and copies ran while one was open for 0% of the time, Pallas kernels for 0%

commit v1 on v0

--- a/solution.py
+++ b/solution.py
@@ -77,7 +77,9 @@
         preferred_element_type=jnp.float32,
     )
     new_master = master * (1.0 - learning_rate * decay_rate) - learning_rate * update
-    weights = lax.all_gather(new_master.astype(jnp.bfloat16), DP, axis=1, tiled=True)
+    part = new_master.astype(jnp.bfloat16)
+    outgoing = jnp.stack([part] * lax.axis_size(DP))
+    weights = jnp.concatenate(lax.all_to_all(outgoing, DP, 0, 0), axis=1)
     return (weights, new_master, new_first, new_second)
 
 

time: 429 us -> 479 us (1.12)
  blocking collectives: 34.8 us -> 136 us
  waiting for transfers between devices: 325 us -> 273 us
    all_to_all x0 -> x1, blocking collectives: none -> 101 us  [per_device(): weights = jnp.concatenate(lax.all_to_all(outgoing, DP, 0, 0), axis=1)]
    all_gather x1 -> x0, waiting for transfers between devices: 52.4 us -> none  [per_device(): lax.all_gather(new_master.astype(jnp.bfloat16), DP, axis=1, tiled=True)]
    all_to_all x0 -> x1, local copies, waits for them, and re-layouts: none -> 8.64 us  [per_device(): weights = jnp.concatenate(lax.all_to_all(outgoing, DP, 0, 0), axis=1)]
    unnamed x15 -> x14, local copies, waits for them, and re-layouts: 7.79 us -> 0.04 us
    unnamed x7 -> x6, waiting for transfers between devices: 46 us -> 46 us
  transfers between devices with their start and end apart: 6 -> 5, of which waited for: 6 -> 5; matrix products, arithmetic and copies ran while one was open for 0% -> 0% of each run, Pallas kernels for 0% -> 0%
where the time goes in v1:
time: 479 us; the launch traced here: 478 us
  waiting for transfers between devices  273 us (57%)
  blocking collectives  136 us (28%)
  local copies, waits for them, and re-layouts  29.8 us (6%)
  matrix products  23.6 us (5%)
  between operations  14.5 us (3%)
    all_to_all x1, blocking collectives, per_device(): weights = jnp.concatenate(lax.all_to_all(outgoing, DP, 0, 0), axis=1)  101 us
    reduce_scatter x1, waiting for transfers between devices, per_device(): lax.psum_scatter(grad_parts[0], DP, scatter_dimension=1, tiled=True)  97.1 us
    all_gather x1, waiting for transfers between devices, per_device(): right_full = lax.all_gather(right_basis, DP, axis=1, tiled=True)  56.5 us
    all_gather x1, waiting for transfers between devices, per_device(): lax.all_gather(back_rows, DP, axis=1, tiled=True)  54.2 us
    unnamed x6, waiting for transfers between devices  46 us
    psum x4, blocking collectives, over_axes(): array = lax.psum(array, axis)  34.8 us
    reduce_scatter x1, waiting for transfers between devices, summed_rows(): parts = lax.psum_scatter(parts, core, scatter_dimension=0, tiled=True)  18.8 us
    optimization_barrier x1, local copies, waits for them, and re-layouts, per_device(): lax.optimization_barrier(raw_term.astype(jnp.bfloat16)).astype(jnp.float32)  11.4 us
  transfers between devices with their start and end apart: 5, of which 5 were waited for; matrix products, arithmetic and copies ran while one was open for 0% of the time, Pallas kernels for 0%

profile of v1, /device:TPU:1, one launch (start us, length us, event | category | flops | bytes accessed | tf_op | source)
XLA Modules:
  0.0 478.3 jit_solution(9779430416640744740)
XLA Ops:
  7.2 0.7 reduce-scatter.6.cloned.1.call-update
  8.0 0.7 all-gather.3.cloned.1.call-update
  8.7 0.0 reduce-scatter.8.cloned.1.call-start
  8.7 97.1 %reduce-scatter.6.cloned.1.call-done = bf16[4,32,1024]{2,1,0:T(8,128)(2,1)} async-done(((bf16[4,1024,1024]{2,1,0:T(8,128)(2,1)}), bf16[4,32,1024]{2,1,0:T(8,128)(2,1)}) %reduce-scatter.6.cloned.1.call-update) | async-done | bytes 262160 | tf_op jit(solution)/shard_map/reduce_scatter | solution.py:40
  105.8 56.5 %all-gather.3.cloned.1.call-done = bf16[4,1024,1024]{2,1,0:T(8,128)(2,1)} async-done(((bf16[4,32,1024]{2,1,0:T(8,128)(2,1)}), bf16[4,1024,1024]{2,1,0:T(8,128)(2,1)}) %all-gather.3.cloned.1.call-update) | async-done | bytes 8388624 | tf_op jit(solution)/shard_map/all_gather | solution.py:46
  162.3 10.8 %convert_bitcast_fusion = bf16[1024,4,1024]{0,2,1:T(8,128)(2,1)} fusion(bf16[4,32,1024]{2,1,0:T(8,128)(2,1)S(1)} %copy-done, bf16[4,32,1024]{2,1,0:T(8,128)(2,1)} %reduce-scatter.6.cloned.1.call-done, bf16[4,1024,1024]{2,1,0:T(8,128)(2,1)} %all-gather.3.cloned.1.call-done), kind=kOutput, calls=%fused_computation | convolution fusion | flops 541196288 | bytes 17301504 | tf_op jit(solution)/shard_map/isx,isb->xib/dot_general | solution.py:51
  173.2 11.4 %copy.16 = bf16[1024,4,1024]{2,0,1:T(8,128)(2,1)} copy(bf16[1024,4,1024]{0,2,1:T(8,128)(2,1)} %convert_bitcast_fusion) | data formatting | bytes 16777216 | tf_op jit(solution)/shard_map/optimization_barrier | solution.py:53
  184.6 8.6 %copy.17 = bf16[2,16,32,4,1024]{4,2,3,1,0:T(8,128)(2,1)} copy(bf16[2,16,32,4,1024]{4,2,0,1,3:T(8,128)(2,1)} %bitcast.27) | data formatting | bytes 16777216 | tf_op jit(solution)/shard_map/transpose | solution.py:34
  193.2 0.0 reduce-scatter.10.cloned.1.call-start
  193.3 18.8 %reduce-scatter.8.cloned.1.call-done = bf16[16,32,4,1024]{3,1,2,0:T(8,128)(2,1)} async-done(((bf16[32,32,4,1024]{3,1,2,0:T(8,128)(2,1)}), bf16[16,32,4,1024]{3,1,2,0:T(8,128)(2,1)}) %reduce-scatter.8.cloned.1.call-update) | async-done | bytes 4194320 | tf_op jit(solution)/shard_map/reduce_scatter | solution.py:35
  212.1 0.0 all-gather.5.cloned.1.call-start
  212.2 0.7 multiply_reduce_fusion
  212.9 9.1 %psum.28 = f32[]{:T(128)} all-reduce(f32[]{:T(128)} %multiply_reduce_fusion), channel_id=1, replica_groups=mesh['dp_0'=4,'dp_1'=4,'dp_2'=2,'mp'=4] {'dp_0'}, use_global_device_ids=true, to_apply=%region_2.0 | all-reduce | flops 1 | bytes 8 | tf_op jit(solution)/shard_map/psum | solution.py:21
  222.0 9.5 %psum.29 = f32[]{:T(128)} all-reduce(f32[]{:T(128)} %psum.28), channel_id=1, replica_groups=mesh['dp_0'=4,'dp_1'=4,'dp_2'=2,'mp'=4] {'dp_1'}, use_global_device_ids=true, to_apply=%region_3.0 | all-reduce | flops 1 | bytes 8 | tf_op jit(solution)/shard_map/psum | solution.py:21
  231.5 6.7 %psum.30 = f32[]{:T(128)} all-reduce(f32[]{:T(128)} %psum.29), channel_id=1, replica_groups=mesh['dp_0'=4,'dp_1'=4,'dp_2'=2,'mp'=4] {'dp_2'}, use_global_device_ids=true, to_apply=%region_4.0 | all-reduce | flops 1 | bytes 8 | tf_op jit(solution)/shard_map/psum | solution.py:21
  238.2 9.5 %psum.31 = f32[]{:T(128)} all-reduce(f32[]{:T(128)} %psum.30), channel_id=1, replica_groups=mesh['dp_0'=4,'dp_1'=4,'dp_2'=2,'mp'=4] {'mp'}, use_global_device_ids=true, to_apply=%region_5.0 | all-reduce | flops 1 | bytes 8 | tf_op jit(solution)/shard_map/psum | solution.py:21
  248.4 44.5 %reduce-scatter.10.cloned.1.call-done = bf16[1,32,4,1024]{3,1,2,0:T(8,128)(2,1)} async-done(((bf16[16,32,4,1024]{3,1,2,0:T(8,128)(2,1)}), bf16[1,32,4,1024]{3,1,2,0:T(8,128)(2,1)}) %reduce-scatter.10.cloned.1.call-update) | async-done | bytes 262160
  292.9 1.1 multiply_add_fusion
  294.1 7.0 %convolution_convert_fusion = bf16[4,32,1024]{2,1,0:T(8,128)(2,1)} fusion(bf16[4,1024,1024]{2,1,0:T(8,128)(2,1)} %all-gather.3.cloned.1.call-done, f32[4,32,1024]{2,1,0:T(8,128)S(1)} %get-tuple-element.5, f32[4,32,1024]{2,1,0:T(8,128)S(1)} %get-tuple-element.4), kind=kOutput, calls=%fused_computation.4 | convolution fusion | flops 269221888 | bytes 9699328 | tf_op jit(solution)/shard_map/isb,icb->isc/dot_general | solution.py:69
  301.2 54.2 %all-gather.5.cloned.1.call-done = bf16[4,1024,1024]{2,1,0:T(8,128)(2,1)} async-done(((bf16[4,32,1024]{2,1,0:T(8,128)(2,1)}), bf16[4,1024,1024]{2,1,0:T(8,128)(2,1)}) %all-gather.5.cloned.1.call-update) | async-done | bytes 8388624 | tf_op jit(solution)/shard_map/all_gather | solution.py:76
  355.4 5.7 %fusion.7 = (bf16[4,32,1024]{2,1,0:T(8,128)(2,1)S(1)}, f32[4,32,1024]{2,1,0:T(8,128)}) fusion(bf16[4,32,1024]{2,1,0:T(8,128)(2,1)S(1)} %copy-done, bf16[4,1024,1024]{2,1,0:T(8,128)(2,1)} %all-gather.5.cloned.1.call-done, f32[4,32,1024]{2,1,0:T(8,128)S(1)} %copy-done.6), kind=kOutput, calls=%fused_computation.16 | convolution fusion | flops 268959744 | bytes 9961472 | tf_op jit(solution)/shard_map/isk,ikc->isc/dot_general | solution.py:73
  361.2 1.1 stack.2
  362.2 100.9 %all_to_all.5 = bf16[32,4,32,1024]{3,2,1,0:T(8,128)(2,1)} all-to-all(bf16[32,4,32,1024]{3,2,1,0:T(8,128)(2,1)S(1)} %stack.2), channel_id=1, replica_groups=mesh['dp_0'=4,'dp_1'=4,'dp_2'=2,'mp'=4] {'dp_0','dp_1','dp_2'}, dimensions={0} | all-to-all | bytes 16777216 | tf_op jit(solution)/shard_map/all_to_all | solution.py:82
  463.2 8.6 %copy.18 = bf16[32,4,32,1024]{3,2,0,1:T(8,128)(2,1)} copy(bf16[32,4,32,1024]{3,2,1,0:T(8,128)(2,1)} %all_to_all.5) | data formatting | bytes 16777216 | tf_op jit(solution)/shard_map/all_to_all | solution.py:82
  (19 shorter events, 0.2 us)
Async XLA Ops:
  7.2 155.2 %copy-start = (bf16[4,32,1024]{2,1,0:T(8,128)(2,1)S(1)}, bf16[4,32,1024]{2,1,0:T(8,128)(2,1)}, u32[]{:S(2)}) copy-start(bf16[4,32,1024]{2,1,0:T(8,128)(2,1)} %param.10) | copy-start | bytes 786436
  7.2 98.6 %reduce-scatter.6.cloned.1.call-start = ((), (), s32[]{:S(2)}) async-start(), calls=%async_computation.4 | async-start | bytes 8650752 | tf_op jit(solution)/shard_map/reduce_scatter | solution.py:40
  7.9 154.4 %all-gather.3.cloned.1.call-start = ((), (), s32[]{:S(2)}) async-start(), calls=%async_computation.5 | async-start | bytes 8650752 | tf_op jit(solution)/shard_map/all_gather | solution.py:46
  8.7 203.4 %reduce-scatter.8.cloned.1.call-start = ((), (), s32[]{:S(2)}) async-start(), calls=%async_computation.6 | async-start | bytes 12582912 | tf_op jit(solution)/shard_map/reduce_scatter | solution.py:35
  193.2 19.0 %copy-start.3 = (bf16[4,32,1024]{2,1,0:T(8,128)(2,1)S(1)}, bf16[4,32,1024]{2,1,0:T(8,128)(2,1)}, u32[]{:S(2)}) copy-start(bf16[4,32,1024]{2,1,0:T(8,128)(2,1)} %reduce-scatter.6.cloned.1.call-done) | copy-start | bytes 786436
  193.2 99.7 %copy-start.4 = (f32[4,32,1024]{2,1,0:T(8,128)S(1)}, f32[4,32,1024]{2,1,0:T(8,128)}, u32[]{:S(2)}) copy-start(f32[4,32,1024]{2,1,0:T(8,128)} %param.8) | copy-start | bytes 1572868
  193.2 99.7 %copy-start.5 = (f32[4,32,1024]{2,1,0:T(8,128)S(1)}, f32[4,32,1024]{2,1,0:T(8,128)}, u32[]{:S(2)}) copy-start(f32[4,32,1024]{2,1,0:T(8,128)} %param.9) | copy-start | bytes 1572868
  193.2 99.7 %reduce-scatter.10.cloned.1.call-start = ((), (), s32[]{:S(2)}) async-start(), calls=%async_computation.8 | async-start | bytes 4456448
  212.1 143.3 %copy-start.6 = (f32[4,32,1024]{2,1,0:T(8,128)S(1)}, f32[4,32,1024]{2,1,0:T(8,128)}, u32[]{:S(2)}) copy-start(f32[4,32,1024]{2,1,0:T(8,128)} %param.7) | copy-start | bytes 1572868
  212.1 143.3 %all-gather.5.cloned.1.call-start = ((), (), s32[]{:S(2)}) async-start(), calls=%async_computation.7 | async-start | bytes 8650752 | tf_op jit(solution)/shard_map/all_gather | solution.py:76
  294.1 67.1 %copy-start.1 = (f32[4,32,1024]{2,1,0:T(8,128)}, f32[4,32,1024]{2,1,0:T(8,128)S(1)}, u32[]{:S(2)}) copy-start(f32[4,32,1024]{2,1,0:T(8,128)S(1)} %get-tuple-element.4) | copy-start | bytes 1572868
  294.1 67.1 %copy-start.2 = (f32[4,32,1024]{2,1,0:T(8,128)}, f32[4,32,1024]{2,1,0:T(8,128)S(1)}, u32[]{:S(2)}) copy-start(f32[4,32,1024]{2,1,0:T(8,128)S(1)} %get-tuple-element.5) | copy-start | bytes 1572868
Sparse Core Ops, SparseCore 0:
  11.7 94.0 reduce-scatter.5
  108.2 54.1 all-gather.2
  193.4 18.6 reduce-scatter.7
  215.3 77.5 reduce-scatter.9
  301.3 54.0 all-gather.4
